TPU v7x, 32 devices: a whole 2x2x4 slice. The times are simulated.
32 devices in a mesh: pp: 2 (over core), ep: 16 (over z, y, x), tp: 1.
Axes of the slice: x: 2, y: 2, z: 4, core: 2. Of those that a mesh axis runs over, the one named last changes fastest.
Arguments:
- acts: bfloat16 [2, 96, 3072], P(None, 'ep'), may hold values from -6 to 6
- route_ids: int32 [2, 2, 96, 8], P('pp', None, 'ep'), may hold values from 0 to 23, all different within a row; in each aligned block of 6 rows (0 to 5, 6 to 11, ..., all dimensions but the last counted through in order) at most 2 rows name the same one
- norm_gain: bfloat16 [2, 3072], P('pp'), may hold values from 0.5 to 1.5
- router: bfloat16 [2, 3072, 24], P('pp'), may hold values from -0.109375 to 0.109375
- dense_gate: bfloat16 [2, 3072, 6144], P('pp', None, ('ep', 'tp')), may hold values from -0.109375 to 0.109375
- dense_up: bfloat16 [2, 3072, 6144], P('pp', None, ('ep', 'tp')), may hold values from -0.109375 to 0.109375
- dense_down: bfloat16 [2, 6144, 3072], P('pp', ('ep', 'tp')), may hold values from -0.078125 to 0.078125
- expert_gate: bfloat16 [2, 16, 3072, 1024], P('pp', 'ep', None, 'tp'), may hold values from -0.109375 to 0.109375
- expert_up: bfloat16 [2, 16, 3072, 1024], P('pp', 'ep', None, 'tp'), may hold values from -0.109375 to 0.109375
- expert_down: bfloat16 [2, 16, 1024, 3072], P('pp', 'ep', 'tp'), may hold values from -0.1875 to 0.1875
Outputs:
- layer_out: bfloat16 [2, 2, 96, 3072], P('pp', None, 'ep')
Inputs may be any that keep to these rules, and one draw needn't show every extreme that they name: `route_ids`: the 8 ids of a token differ. In each layer and microbatch, among the 6 tokens of one ep index no id is named by more than 2 tokens, a bound that some block reaches.
All inputs are finite; a program needn't handle non-finite values.
Results may differ from a plain program's by a relative error of at most 0.008.
Values may be sent and summed in bfloat16 or wider, within the bound.
No kernel may reach another device: no remote copies, remote signals or barrier semaphores. Data moves between devices by JAX's collectives and lax.ppermute only.
A program may use at most 128 MiB of HBM per device.

v0:
```python
import jax
import jax.numpy as jnp
from jax import lax
from jax.sharding import PartitionSpec as P


def from_behind(block, axis, distance):
    devices = range(lax.axis_size(axis))
    route = [(i - distance, i) for i in devices if i - distance in devices]
    return lax.ppermute(block, axis, route)


def normalize(inputs, gain):
    widened = inputs.astype(jnp.float32)
    spread = jnp.mean(widened * widened, axis=-1, keepdims=True)
    normed = (widened * lax.rsqrt(spread + 1e-06) * gain.astype(jnp.float32)).astype(jnp.bfloat16)
    return (widened, normed)


def gated_block(inputs, w_gate, w_up, w_down):
    gate_part = jnp.dot(inputs, w_gate, preferred_element_type=jnp.float32)
    up_part = jnp.dot(inputs, w_up, preferred_element_type=jnp.float32)
    hidden = (jax.nn.silu(gate_part) * up_part).astype(jnp.bfloat16)
    return jnp.dot(hidden, w_down, preferred_element_type=jnp.float32)


def choice_weights(normed, route_rows, router_w, n_real):
    n_total = router_w.shape[1]
    gates = jax.nn.sigmoid(jnp.dot(normed, router_w, preferred_element_type=jnp.float32))
    picked = (route_rows[:, :, None] == jnp.arange(n_total, dtype=jnp.int32)[None, None, :]).astype(
        jnp.float32
    )
    weights = jnp.sum(picked * gates[:, None, :], axis=-1)
    zero_share = jnp.sum(jnp.where(route_rows >= n_real, weights, jnp.float32(0.0)), axis=-1)
    return (weights, picked, zero_share)


def on_device(
    acts,
    route_ids,
    norm_gain,
    router,
    dense_gate,
    dense_up,
    dense_down,
    expert_gate,
    expert_up,
    expert_down,
):
    n_micro, per_group, width = acts.shape
    top_count = route_ids.shape[-1]
    n_groups = lax.axis_size("ep")
    n_pairs = lax.axis_size("tp")
    section = lax.axis_index("pp")
    group_pos = lax.axis_index("ep")
    pair_pos = lax.axis_index("tp")
    micro_rows = per_group * n_groups
    share = per_group // n_pairs
    gain = norm_gain[0]
    router_w = router[0]
    total_ids = router_w.shape[1]
    slot_count = max(2, (per_group * top_count + total_ids - 1) // total_ids)
    d_gate = dense_gate[0]
    d_up = dense_up[0]
    d_down = dense_down[0]
    e_gate = expert_gate[0, 0]
    e_up = expert_up[0, 0]
    e_down = expert_down[0, 0]
    slot_range = jnp.arange(slot_count, dtype=jnp.float32)
    incoming = jnp.zeros((per_group, width), jnp.bfloat16)
    outputs = jnp.zeros((n_micro, per_group, width), jnp.bfloat16)
    for tick_index in range(n_micro + 1):
        local_micro = tick_index - section
        micro_index = jnp.clip(local_micro, 0, n_micro - 1)
        valid = jnp.logical_and(local_micro >= 0, local_micro < n_micro)
        first_input = acts[min(tick_index, n_micro - 1)]
        current = jnp.where(section == 0, first_input, incoming)
        route_rows = lax.dynamic_index_in_dim(route_ids[0], micro_index, 0, keepdims=False)
        widened, normed = normalize(current, gain)
        weights, picked, zero_share = choice_weights(normed, route_rows, router_w, n_groups)
        all_normed = lax.all_gather(normed, "ep", axis=0, tiled=True)
        real_pick = picked[:, :, :n_groups]
        hot = jnp.sum(real_pick, axis=1)
        coef = jnp.einsum("tk,tke->te", weights, real_pick, precision=lax.Precision.HIGHEST)
        position = jnp.cumsum(hot, axis=0) - hot
        select = hot.T[:, None, :] * (position.T[:, None, :] == slot_range[None, :, None]).astype(
            jnp.float32
        )
        outgoing = jnp.einsum(
            "esi,id->esd", select.astype(jnp.bfloat16), normed, preferred_element_type=jnp.float32
        ).astype(jnp.bfloat16)
        received = lax.all_to_all(outgoing, "ep", split_axis=0, concat_axis=0, tiled=True)
        flat = received.reshape(-1, width)
        produced = gated_block(flat, e_gate, e_up, e_down).reshape(received.shape[:-1] + (width,))
        returned = lax.all_to_all(produced, "ep", split_axis=0, concat_axis=0, tiled=True)
        own_rows = jnp.einsum(
            "esi,esd->id", select * coef.T[:, None, :], returned, precision=lax.Precision.HIGHEST
        )
        extra = lax.dynamic_update_slice_in_dim(
            jnp.zeros((micro_rows, width), jnp.float32), own_rows, group_pos * per_group, 0
        )
        summed = lax.psum_scatter(
            gated_block(all_normed, d_gate, d_up, d_down) + extra,
            ("ep", "tp"),
            scatter_dimension=0,
            tiled=True,
        )
        offset = pair_pos * share
        own_inputs = lax.dynamic_slice_in_dim(widened, offset, share, 0)
        own_normed = lax.dynamic_slice_in_dim(normed, offset, share, 0).astype(jnp.float32)
        own_zero = lax.dynamic_slice_in_dim(zero_share, offset, share, 0)
        result_part = (own_inputs + summed + own_zero[:, None] * own_normed).astype(jnp.bfloat16)
        finished = lax.all_gather(result_part, "tp", axis=0, tiled=True)
        updated = lax.dynamic_update_index_in_dim(outputs, finished, micro_index, 0)
        outputs = jnp.where(valid, updated, outputs)
        if tick_index < n_micro:
            incoming = from_behind(finished, "pp", 1)
    return outputs[None]


def solution(mesh):
    return jax.shard_map(
        on_device,
        mesh=mesh,
        in_specs=(
            P(None, "ep", None),
            P("pp", None, "ep", None),
            P("pp", None),
            P("pp", None, None),
            P("pp", None, ("ep", "tp")),
            P("pp", None, ("ep", "tp")),
            P("pp", ("ep", "tp"), None),
            P("pp", "ep", None, "tp"),
            P("pp", "ep", None, "tp"),
            P("pp", "ep", "tp", None),
        ),
        out_specs=P("pp", None, "ep", None),
        check_vma=False,
    )
```

profile of v0, /device:TPU:0, one launch (start us, length us, event | category | flops | bytes accessed | tf_op | source)
XLA Modules:
  0.0 461.7 jit_solution(911177788010176452)
XLA Ops:
  4.8 8.3 %all-to-all-start = ((bf16[16,2,3072]{2,1,0:T(2,128)(2,1)}), bf16[16,2,3072]{2,1,0:T(2,128)(2,1)S(1)}, u32[]{:S(2)}, u32[]{:S(2)}) async-start(bf16[16,2,3072]{2,1,0:T(2,128)(2,1)} %copy.46), calls=%async_computation | async-start | bytes 393216 | tf_op jit(solution)/shard_map/all_to_all | solution.py:92
  15.1 48.1 %all-gather = bf16[16,6,3072]{2,1,0:T(8,128)(2,1)} all-gather(bf16[1,6,3072]{2,1,0:T(8,128)(2,1)S(1)} %fusion.192), channel_id=1, replica_groups=mesh['pp'=2,'ep'=16,'tp'=1] {'ep'}, dimensions={0}, use_global_device_ids=true | all-gather | bytes 626688 | tf_op jit(solution)/shard_map/all_gather | solution.py:81
  63.3 4.1 fusion.19
  69.2 4.0 fusion.7
  74.2 3.6 all-to-all-start.1
  81.0 2.9 fusion.40
  83.9 3.8 fusion.28
  90.7 50.0 %fusion = f32[8,3072]{1,0:T(8,128)S(1)} fusion(f32[96,3072]{1,0:T(8,128)} %add.116), kind=kCustom, calls=%all-reduce-scatter | all-reduce-scatter fusion | flops 393217 | bytes 1278464
  143.8 5.1 %collective-permute-start.4 = (f32[8,3072]{1,0:T(8,128)S(1)}, f32[8,3072]{1,0:T(8,128)S(1)}, u32[]{:S(2)}, u32[]{:S(2)}) collective-permute-start(f32[8,3072]{1,0:T(8,128)S(1)} %fusion), channel_id=1, source_target_pairs={{0,3},{1,4},{2,5},{3,6},{4,7},{5,8},{6,9},{7,10},{8,11},{9,12},{10... | collective-permute-start | bytes 294920
  148.9 3.3 collective-permute-start.5
  161.3 4.7 %all-to-all-start.2 = ((bf16[16,2,3072]{2,1,0:T(2,128)(2,1)}), bf16[16,2,3072]{2,1,0:T(2,128)(2,1)S(1)}, u32[]{:S(2)}, u32[]{:S(2)}) async-start(bf16[16,2,3072]{2,1,0:T(2,128)(2,1)} %copy.52), calls=%async_computation.2 | async-start | bytes 393216 | tf_op jit(solution)/shard_map/all_to_all | solution.py:92
  166.1 48.3 %all-gather.1 = bf16[16,6,3072]{2,1,0:T(8,128)(2,1)} all-gather(bf16[1,6,3072]{2,1,0:T(8,128)(2,1)S(1)} %fusion.198), channel_id=1, replica_groups=mesh['pp'=2,'ep'=16,'tp'=1] {'ep'}, dimensions={0}, use_global_device_ids=true | all-gather | bytes 626688 | tf_op jit(solution)/shard_map/all_gather | solution.py:81
  214.5 4.0 fusion.17
  218.5 4.0 fusion.72
  222.5 4.0 fusion.5
  227.5 3.7 all-to-all-start.3
  232.8 2.8 fusion.38
  235.6 3.8 fusion.26
  243.9 49.4 %fusion.1 = f32[8,3072]{1,0:T(8,128)S(1)} fusion(f32[96,3072]{1,0:T(8,128)} %add.123), kind=kCustom, calls=%all-reduce-scatter.1 | all-reduce-scatter fusion | flops 393217 | bytes 1278464
  295.9 4.6 collective-permute-start.8
  300.5 2.8 collective-permute-start.9
  313.3 5.3 %all-to-all-start.4 = ((bf16[16,2,3072]{2,1,0:T(2,128)(2,1)}), bf16[16,2,3072]{2,1,0:T(2,128)(2,1)S(1)}, u32[]{:S(2)}, u32[]{:S(2)}) async-start(bf16[16,2,3072]{2,1,0:T(2,128)(2,1)} %copy.57), calls=%async_computation.4 | async-start | bytes 393216 | tf_op jit(solution)/shard_map/all_to_all | solution.py:92
  318.8 48.3 %all-gather.2 = bf16[16,6,3072]{2,1,0:T(8,128)(2,1)} all-gather(bf16[1,6,3072]{2,1,0:T(8,128)(2,1)S(1)} %fusion.195), channel_id=1, replica_groups=mesh['pp'=2,'ep'=16,'tp'=1] {'ep'}, dimensions={0}, use_global_device_ids=true | all-gather | bytes 626688 | tf_op jit(solution)/shard_map/all_gather | solution.py:81
  367.1 4.0 fusion.15
  371.1 4.0 fusion.69
  375.1 4.0 fusion.3
  380.2 3.6 all-to-all-start.5
  385.2 2.9 fusion.36
  388.1 3.8 fusion.24
  396.3 49.4 %fusion.2 = f32[8,3072]{1,0:T(8,128)S(1)} fusion(f32[96,3072]{1,0:T(8,128)} %add.130), kind=kCustom, calls=%all-reduce-scatter.2 | all-reduce-scatter fusion | flops 393217 | bytes 1278464
  448.3 4.6 collective-permute-start.12
  452.9 2.7 collective-permute-start.13
  (133 shorter events, 63.0 us)
Async XLA Ops:
  0.0 83.9 %copy-start = (bf16[1,384,3072]{2,1,0:T(8,128)(2,1)S(1)}, bf16[1,384,3072]{2,1,0:T(8,128)(2,1)}, u32[]{:S(2)}) copy-start(bf16[1,384,3072]{2,1,0:T(8,128)(2,1)} %param.16) | copy-start | bytes 7077892
  2.9 10.3 %copy-start.9 = (f32[6]{0:T(128)}, f32[6]{0:T(128)S(1)}, u32[]{:S(2)}) copy-start(f32[6]{0:T(128)S(1)} %add_rsqrt_fusion.2) | copy-start | bytes 76
  4.8 58.4 %all-to-all-start = ((bf16[16,2,3072]{2,1,0:T(2,128)(2,1)}), bf16[16,2,3072]{2,1,0:T(2,128)(2,1)S(1)}, u32[]{:S(2)}, u32[]{:S(2)}) async-start(bf16[16,2,3072]{2,1,0:T(2,128)(2,1)} %copy.46), calls=%async_computation | async-start | bytes 393216 | tf_op jit(solution)/shard_map/all_to_all | solution.py:92
  63.3 4.6 copy-start.1
  73.1 6.7 %copy-start.12 = (u32[32]{0:T(128)S(1)}, u32[32]{0:T(128)}, u32[]{:S(2)}) copy-start(u32[32]{0:T(128)} %constant.91) | copy-start | bytes 388
  74.2 13.5 %all-to-all-start.1 = ((f32[16,2,3072]{2,1,0:T(2,128)}), f32[16,2,3072]{2,1,0:T(2,128)S(1)}, u32[]{:S(2)}, u32[]{:S(2)}) async-start(f32[16,2,3072]{2,1,0:T(2,128)} %copy.48), calls=%async_computation.1 | async-start | bytes 786432 | tf_op jit(solution)/shard_map/all_to_all | solution.py:95
  140.7 13.7 %collective-permute-start.2 = (f32[8,3072]{1,0:T(8,128)S(1)}, f32[8,3072]{1,0:T(8,128)S(1)}, u32[]{:S(2)}, u32[]{:S(2)}) collective-permute-start(f32[8,3072]{1,0:T(8,128)S(1)} %fusion), channel_id=1, source_target_pairs={{0,1},{1,2},{2,3},{3,4},{4,5},{5,6},{6,7},{7,8},{8,9},{9,10},{10,1... | collective-permute-start | bytes 294920
  142.5 11.9 %collective-permute-start.3 = (f32[8,3072]{1,0:T(8,128)S(1)}, f32[8,3072]{1,0:T(8,128)S(1)}, u32[]{:S(2)}, u32[]{:S(2)}) collective-permute-start(f32[8,3072]{1,0:T(8,128)S(1)} %fusion), channel_id=1, source_target_pairs={{0,2},{1,3},{2,4},{3,5},{4,6},{5,7},{6,8},{7,9},{8,10},{9,11},{10,... | collective-permute-start | bytes 294920
  143.8 10.6 %collective-permute-start.4 = (f32[8,3072]{1,0:T(8,128)S(1)}, f32[8,3072]{1,0:T(8,128)S(1)}, u32[]{:S(2)}, u32[]{:S(2)}) collective-permute-start(f32[8,3072]{1,0:T(8,128)S(1)} %fusion), channel_id=1, source_target_pairs={{0,3},{1,4},{2,5},{3,6},{4,7},{5,8},{6,9},{7,10},{8,11},{9,12},{10... | collective-permute-start | bytes 294920
  148.9 5.5 %collective-permute-start.5 = (f32[6,3072]{1,0:T(8,128)S(1)}, f32[6,3072]{1,0:T(8,128)S(1)}, u32[]{:S(2)}, u32[]{:S(2)}) collective-permute-start(f32[6,3072]{1,0:T(8,128)S(1)} %slice.36), channel_id=1, source_target_pairs={{0,4},{1,5},{2,6},{3,7},{4,8},{5,9},{6,10},{7,11},{8,12},{9,13},{1... | collective-permute-start | bytes 221192
  155.7 2.2 collective-permute-start
  158.9 2.4 copy-start.10
  161.3 53.1 %all-to-all-start.2 = ((bf16[16,2,3072]{2,1,0:T(2,128)(2,1)}), bf16[16,2,3072]{2,1,0:T(2,128)(2,1)S(1)}, u32[]{:S(2)}, u32[]{:S(2)}) async-start(bf16[16,2,3072]{2,1,0:T(2,128)(2,1)} %copy.52), calls=%async_computation.2 | async-start | bytes 393216 | tf_op jit(solution)/shard_map/all_to_all | solution.py:92
  166.1 65.1 %copy-start.7 = (f32[6,8]{1,0:T(8,128)}, f32[6,8]{1,0:T(8,128)S(1)}, u32[]{:S(2)}) copy-start(f32[6,8]{1,0:T(8,128)S(1)} %select_reduce_fusion.1) | copy-start | bytes 580
  227.5 13.3 %all-to-all-start.3 = ((f32[16,2,3072]{2,1,0:T(2,128)}), f32[16,2,3072]{2,1,0:T(2,128)S(1)}, u32[]{:S(2)}, u32[]{:S(2)}) async-start(f32[16,2,3072]{2,1,0:T(2,128)} %copy.54), calls=%async_computation.3 | async-start | bytes 786432 | tf_op jit(solution)/shard_map/all_to_all | solution.py:95
  235.6 67.6 %copy-start.8 = (f32[6,8]{1,0:T(8,128)S(1)}, f32[6,8]{1,0:T(8,128)}, u32[]{:S(2)}) copy-start(f32[6,8]{1,0:T(8,128)} %copy-done.7) | copy-start | bytes 580
  239.5 69.0 %copy-start.11 = (f32[6]{0:T(128)S(1)}, f32[6]{0:T(128)}, u32[]{:S(2)}) copy-start(f32[6]{0:T(128)} %copy-done.10) | copy-start | bytes 76
  242.2 68.5 %copy-start.2 = (bf16[1,6,3072]{2,0,1:T(2,128)(2,1)S(1)}, bf16[1,6,3072]{2,0,1:T(2,128)(2,1)}, u32[]{:S(2)}) copy-start(bf16[1,6,3072]{2,0,1:T(2,128)(2,1)} %get-tuple-element.15) | copy-start | bytes 110596
  293.3 12.2 %collective-permute-start.6 = (f32[8,3072]{1,0:T(8,128)S(1)}, f32[8,3072]{1,0:T(8,128)S(1)}, u32[]{:S(2)}, u32[]{:S(2)}) collective-permute-start(f32[8,3072]{1,0:T(8,128)S(1)} %fusion.1), channel_id=1, source_target_pairs={{0,1},{1,2},{2,3},{3,4},{4,5},{5,6},{6,7},{7,8},{8,9},{9,10},{10,1... | collective-permute-start | bytes 294920
  294.6 10.9 %collective-permute-start.7 = (f32[8,3072]{1,0:T(8,128)S(1)}, f32[8,3072]{1,0:T(8,128)S(1)}, u32[]{:S(2)}, u32[]{:S(2)}) collective-permute-start(f32[8,3072]{1,0:T(8,128)S(1)} %fusion.1), channel_id=1, source_target_pairs={{0,2},{1,3},{2,4},{3,5},{4,6},{5,7},{6,8},{7,9},{8,10},{9,11},{10,... | collective-permute-start | bytes 294920
  295.9 10.2 %collective-permute-start.8 = (f32[8,3072]{1,0:T(8,128)S(1)}, f32[8,3072]{1,0:T(8,128)}, u32[]{:S(2)}, u32[]{:S(2)}) collective-permute-start(f32[8,3072]{1,0:T(8,128)S(1)} %fusion.1), channel_id=1, source_target_pairs={{0,3},{1,4},{2,5},{3,6},{4,7},{5,8},{6,9},{7,10},{8,11},{9,12},{10... | collective-permute-start | bytes 294920
  300.5 5.0 %collective-permute-start.9 = (f32[6,3072]{1,0:T(8,128)S(1)}, f32[6,3072]{1,0:T(8,128)S(1)}, u32[]{:S(2)}, u32[]{:S(2)}) collective-permute-start(f32[6,3072]{1,0:T(8,128)S(1)} %slice.37), channel_id=1, source_target_pairs={{0,4},{1,5},{2,6},{3,7},{4,8},{5,9},{6,10},{7,11},{8,12},{9,13},{1... | collective-permute-start | bytes 221192
  305.4 0.6 copy-start.4
  308.6 2.2 collective-permute-start.1
  313.3 53.8 %all-to-all-start.4 = ((bf16[16,2,3072]{2,1,0:T(2,128)(2,1)}), bf16[16,2,3072]{2,1,0:T(2,128)(2,1)S(1)}, u32[]{:S(2)}, u32[]{:S(2)}) async-start(bf16[16,2,3072]{2,1,0:T(2,128)(2,1)} %copy.57), calls=%async_computation.4 | async-start | bytes 393216 | tf_op jit(solution)/shard_map/all_to_all | solution.py:92
  380.2 13.2 %all-to-all-start.5 = ((f32[16,2,3072]{2,1,0:T(2,128)}), f32[16,2,3072]{2,1,0:T(2,128)S(1)}, u32[]{:S(2)}, u32[]{:S(2)}) async-start(f32[16,2,3072]{2,1,0:T(2,128)} %copy.59), calls=%async_computation.5 | async-start | bytes 786432 | tf_op jit(solution)/shard_map/all_to_all | solution.py:95
  394.7 66.2 %copy-start.3 = (bf16[1,2,6,3072]{3,2,1,0:T(8,128)(2,1)S(1)}, bf16[1,2,6,3072]{3,2,1,0:T(8,128)(2,1)}, u32[]{:S(2)}) copy-start(bf16[1,2,6,3072]{3,2,1,0:T(8,128)(2,1)} %copy.121) | copy-start | bytes 221188
  445.7 12.1 %collective-permute-start.10 = (f32[8,3072]{1,0:T(8,128)S(1)}, f32[8,3072]{1,0:T(8,128)S(1)}, u32[]{:S(2)}, u32[]{:S(2)}) collective-permute-start(f32[8,3072]{1,0:T(8,128)S(1)} %fusion.2), channel_id=1, source_target_pairs={{0,1},{1,2},{2,3},{3,4},{4,5},{5,6},{6,7},{7,8},{8,9},{9,10},{10,1... | collective-permute-start | bytes 294920
  447.0 10.8 %collective-permute-start.11 = (f32[8,3072]{1,0:T(8,128)S(1)}, f32[8,3072]{1,0:T(8,128)S(1)}, u32[]{:S(2)}, u32[]{:S(2)}) collective-permute-start(f32[8,3072]{1,0:T(8,128)S(1)} %fusion.2), channel_id=1, source_target_pairs={{0,2},{1,3},{2,4},{3,5},{4,6},{5,7},{6,8},{7,9},{8,10},{9,11},{10,... | collective-permute-start | bytes 294920
  448.3 10.2 %collective-permute-start.12 = (f32[8,3072]{1,0:T(8,128)S(1)}, f32[8,3072]{1,0:T(8,128)}, u32[]{:S(2)}, u32[]{:S(2)}) collective-permute-start(f32[8,3072]{1,0:T(8,128)S(1)} %fusion.2), channel_id=1, source_target_pairs={{0,3},{1,4},{2,5},{3,6},{4,7},{5,8},{6,9},{7,10},{8,11},{9,12},{10... | collective-permute-start | bytes 294920
  452.9 4.9 %collective-permute-start.13 = (f32[6,3072]{1,0:T(8,128)S(1)}, f32[6,3072]{1,0:T(8,128)S(1)}, u32[]{:S(2)}, u32[]{:S(2)}) collective-permute-start(f32[6,3072]{1,0:T(8,128)S(1)} %slice.38), channel_id=1, source_target_pairs={{0,4},{1,5},{2,6},{3,7},{4,8},{5,9},{6,10},{7,11},{8,12},{9,13},{1... | collective-permute-start | bytes 221192
  457.8 0.6 copy-start.5
  (1 other events, 0.6 us)
where the time goes:
time: 464 us; the launch traced here: 462 us
  blocking collectives  293 us (63%)
  starting transfers between devices  63.1 us (14%)
  matrix products  61.8 us (13%)
  local copies, waits for them, and re-layouts  27.9 us (6%)
  waiting for transfers between devices  9.39 us (2%)
  other arithmetic  5.04 us (1%)
    unnamed x3, blocking collectives  149 us
    all_gather x3, blocking collectives, on_device(): all_normed = lax.all_gather(normed, 'ep', axis=0, tiled=True)  145 us
    unnamed x12, starting transfers between devices  31.3 us
    dot_general x6, matrix products, gated_block(): return jnp.dot(hidden, w_down, preferred_element_type=jnp.float32)  23.4 us
    dot_general x6, matrix products, gated_block(): gate_part = jnp.dot(inputs, w_gate, preferred_element_type=jnp.float32)  20.6 us
    all_to_all x3, starting transfers between devices, on_device(): lax.all_to_all(outgoing, 'ep', split_axis=0, concat_axis=0, tiled=True)  18.3 us
    unnamed x38, local copies, waits for them, and re-layouts  12.9 us
    all_to_all x3, starting transfers between devices, on_device(): lax.all_to_all(produced, 'ep', split_axis=0, concat_axis=0, tiled=True)  10.8 us
  transfers between devices with their start and end apart: 20, of which 7 were waited for; matrix products, arithmetic and copies ran while one was open for 6% of the time, Pallas kernels for 0%

commit v1 on v0

--- a/solution.py
+++ b/solution.py
@@ -78,7 +78,9 @@
         route_rows = lax.dynamic_index_in_dim(route_ids[0], micro_index, 0, keepdims=False)
         widened, normed = normalize(current, gain)
         weights, picked, zero_share = choice_weights(normed, route_rows, router_w, n_groups)
-        all_normed = lax.all_gather(normed, "ep", axis=0, tiled=True)
+        all_normed = jnp.concatenate(
+            lax.all_to_all(jnp.stack([normed] * lax.axis_size("ep")), "ep", 0, 0), axis=0
+        )
         real_pick = picked[:, :, :n_groups]
         hot = jnp.sum(real_pick, axis=1)
         coef = jnp.einsum("tk,tke->te", weights, real_pick, precision=lax.Precision.HIGHEST)

time: 464 us -> 396 us (0.85)
  blocking collectives: 293 us -> 148 us
  waiting for transfers between devices: 9.39 us -> 53.1 us
  starting transfers between devices: 63.1 us -> 81.5 us
  local copies, waits for them, and re-layouts: 27.9 us -> 37.5 us
    all_gather x3 -> x0, blocking collectives: 145 us -> none  [on_device(): all_normed = lax.all_gather(normed, 'ep', axis=0, tiled=True)]
    all_to_all x3, waiting for transfers between devices: 0.01 us -> 22 us  [on_device(): lax.all_to_all(outgoing, 'ep', split_axis=0, concat_axis=0, tiled=True)]
    all_to_all x0 -> x3, waiting for transfers between devices: none -> 17.9 us  [on_device(): lax.all_to_all(jnp.stack([normed] * lax.axis_size('ep')), 'ep', 0, 0)]
    all_to_all x0 -> x3, starting transfers between devices: none -> 11 us  [on_device(): lax.all_to_all(jnp.stack([normed] * lax.axis_size('ep')), 'ep', 0, 0)]
    all_to_all x3, waiting for transfers between devices: 2.82 us -> 8.1 us  [on_device(): lax.all_to_all(produced, 'ep', split_axis=0, concat_axis=0, tiled=True)]
    unnamed x38 -> x95, local copies, waits for them, and re-layouts: 12.9 us -> 13.1 us
  transfers between devices with their start and end apart: 20 -> 23, of which waited for: 7 -> 13; matrix products, arithmetic and copies ran while one was open for 6% -> 18% of each run, Pallas kernels for 0% -> 0%
where the time goes in v1:
time: 396 us; the launch traced here: 392 us
  blocking collectives  148 us (37%)
  starting transfers between devices  81.5 us (21%)
  matrix products  60.3 us (15%)
  waiting for transfers between devices  53.1 us (13%)
  local copies, waits for them, and re-layouts  37.5 us (9%)
  other arithmetic  9.59 us (2%)
    unnamed x3, blocking collectives  148 us
    unnamed x12, starting transfers between devices  30.6 us
    dot_general x6, matrix products, gated_block(): return jnp.dot(hidden, w_down, preferred_element_type=jnp.float32)  23.6 us
    all_to_all x3, starting transfers between devices, on_device(): lax.all_to_all(outgoing, 'ep', split_axis=0, concat_axis=0, tiled=True)  22.3 us
    all_to_all x3, waiting for transfers between devices, on_device(): lax.all_to_all(outgoing, 'ep', split_axis=0, concat_axis=0, tiled=True)  22 us
    dot_general x6, matrix products, gated_block(): gate_part = jnp.dot(inputs, w_gate, preferred_element_type=jnp.float32)  18.6 us
    all_to_all x3, waiting for transfers between devices, on_device(): lax.all_to_all(jnp.stack([normed] * lax.axis_size('ep')), 'ep', 0, 0)  17.9 us
    all_to_all x3, starting transfers between devices, on_device(): lax.all_to_all(produced, 'ep', split_axis=0, concat_axis=0, tiled=True)  14.9 us
  transfers between devices with their start and end apart: 23, of which 13 were waited for; matrix products, arithmetic and copies ran while one was open for 18% of the time, Pallas kernels for 0%

profile of v1, /device:TPU:0, one launch (start us, length us, event | category | flops | bytes accessed | tf_op | source)
XLA Modules:
  0.0 392.0 jit_solution(9857709186479803796)
XLA Ops:
  5.3 8.3 %all-to-all-start.1 = ((bf16[16,2,3072]{2,1,0:T(2,128)(2,1)}), bf16[16,2,3072]{2,1,0:T(2,128)(2,1)S(1)}, u32[]{:S(2)}, u32[]{:S(2)}) async-start(bf16[16,2,3072]{2,1,0:T(2,128)(2,1)} %copy.46), calls=%async_computation.1 | async-start | bytes 393216 | tf_op jit(solution)/shard_map/all_to_all | solution.py:94
  15.3 7.0 %all-to-all-done.1 = bf16[16,2,3072]{2,1,0:T(2,128)(2,1)S(1)} async-done(((bf16[16,2,3072]{2,1,0:T(2,128)(2,1)}), bf16[16,2,3072]{2,1,0:T(2,128)(2,1)S(1)}, u32[]{:S(2)}, u32[]{:S(2)}) %all-to-all-start.1) | async-done | bytes 196640 | tf_op jit(solution)/shard_map/all_to_all | solution.py:94
  23.2 3.6 all-to-all-start
  27.9 4.1 %fusion.19 = f32[32,1024]{1,0:T(8,128)S(1)} fusion(bf16[32,3072]{1,0:T(8,128)(2,1)S(1)} %reshape.117, bf16[1,1,3072,1024]{3,2,1,0:T(8,128)(2,1)} %param.17), kind=kOutput, calls=%fused_computation.16 | convolution fusion | flops 201326592 | bytes 6619136 | tf_op jit(solution)/shard_map/dot_general | solution.py:21
  33.8 4.0 %fusion.7 = f32[16,2,3072]{2,0,1:T(8,128)S(1)} fusion(bf16[1,1,1024,3072]{3,2,1,0:T(8,128)(2,1)} %param.19, bf16[16,2,1024]{2,1,0:T(2,128)(2,1)S(1)} %dot_general.111), kind=kOutput, calls=%fused_computation.4 | convolution fusion | flops 201326592 | bytes 6750208 | tf_op jit(solution)/shard_map/dot_general | solution.py:24
  38.8 7.1 %all-to-all-done = bf16[16,6,3072]{2,1,0:T(8,128)(2,1)S(1)} async-done(((bf16[16,6,3072]{2,1,0:T(8,128)(2,1)}), bf16[16,6,3072]{2,1,0:T(8,128)(2,1)S(1)}, u32[]{:S(2)}, u32[]{:S(2)}) %all-to-all-start) | async-done | bytes 589856 | tf_op jit(solution)/shard_map/all_to_all | solution.py:82
  45.9 5.0 %all-to-all-start.2 = ((f32[16,2,3072]{2,1,0:T(2,128)}), f32[16,2,3072]{2,1,0:T(2,128)}, u32[]{:S(2)}, u32[]{:S(2)}) async-start(f32[16,2,3072]{2,1,0:T(2,128)} %copy.48), calls=%async_computation.2 | async-start | bytes 786432 | tf_op jit(solution)/shard_map/all_to_all | solution.py:97
  56.0 3.9 fusion.28
  65.7 49.3 %fusion = f32[8,3072]{1,0:T(8,128)S(1)} fusion(f32[96,3072]{1,0:T(8,128)} %add.116), kind=kCustom, calls=%all-reduce-scatter | all-reduce-scatter fusion | flops 393217 | bytes 1278464
  115.1 3.6 collective-permute-start.2
  121.9 3.6 collective-permute-start.5
  135.9 6.4 %all-to-all-start.4 = ((bf16[16,2,3072]{2,1,0:T(2,128)(2,1)}), bf16[16,2,3072]{2,1,0:T(2,128)(2,1)S(1)}, u32[]{:S(2)}, u32[]{:S(2)}) async-start(bf16[16,2,3072]{2,1,0:T(2,128)(2,1)} %copy.52), calls=%async_computation.4 | async-start | bytes 393216 | tf_op jit(solution)/shard_map/all_to_all | solution.py:94
  143.4 8.1 %all-to-all-done.4 = bf16[16,2,3072]{2,1,0:T(2,128)(2,1)S(1)} async-done(((bf16[16,2,3072]{2,1,0:T(2,128)(2,1)}), bf16[16,2,3072]{2,1,0:T(2,128)(2,1)S(1)}, u32[]{:S(2)}, u32[]{:S(2)}) %all-to-all-start.4) | async-done | bytes 196640 | tf_op jit(solution)/shard_map/all_to_all | solution.py:94
  152.5 3.8 all-to-all-start.3
  157.3 4.0 %fusion.17 = f32[32,1024]{1,0:T(8,128)S(1)} fusion(bf16[32,3072]{1,0:T(8,128)(2,1)S(1)} %reshape.119, bf16[1,1,3072,1024]{3,2,1,0:T(8,128)(2,1)} %param.17), kind=kOutput, calls=%fused_computation.14 | convolution fusion | flops 201326592 | bytes 6619136 | tf_op jit(solution)/shard_map/dot_general | solution.py:21
  161.3 4.0 %fusion.72 = bf16[32,1024]{1,0:T(8,128)(2,1)S(1)} fusion(bf16[32,3072]{1,0:T(8,128)(2,1)S(1)} %reshape.119, bf16[1,1,3072,1024]{3,2,1,0:T(8,128)(2,1)} %param.18, f32[32,1024]{1,0:T(8,128)S(1)} %fusion.17), kind=kOutput, calls=%fused_computation.55 | convolution fusion | flops 201523200 | bytes 6684672 | tf_op jit(solution)/shard_map/dot_general | solution.py:22
  165.3 4.0 %fusion.5 = f32[16,2,3072]{2,0,1:T(8,128)S(1)} fusion(bf16[1,1,1024,3072]{3,2,1,0:T(8,128)(2,1)} %param.19, bf16[16,2,1024]{2,1,0:T(2,128)(2,1)S(1)} %dot_general.123), kind=kOutput, calls=%fused_computation.2 | convolution fusion | flops 201326592 | bytes 6750208 | tf_op jit(solution)/shard_map/dot_general | solution.py:24
  170.3 4.8 %all-to-all-done.3 = bf16[16,6,3072]{2,1,0:T(8,128)(2,1)S(1)} async-done(((bf16[16,6,3072]{2,1,0:T(8,128)(2,1)}), bf16[16,6,3072]{2,1,0:T(8,128)(2,1)S(1)}, u32[]{:S(2)}, u32[]{:S(2)}) %all-to-all-start.3) | async-done | bytes 589856 | tf_op jit(solution)/shard_map/all_to_all | solution.py:82
  175.2 5.0 %all-to-all-start.5 = ((f32[16,2,3072]{2,1,0:T(2,128)}), f32[16,2,3072]{2,1,0:T(2,128)S(1)}, u32[]{:S(2)}, u32[]{:S(2)}) async-start(f32[16,2,3072]{2,1,0:T(2,128)} %copy.54), calls=%async_computation.5 | async-start | bytes 786432 | tf_op jit(solution)/shard_map/all_to_all | solution.py:97
  185.1 3.9 fusion.26
  194.8 49.5 %fusion.1 = f32[8,3072]{1,0:T(8,128)S(1)} fusion(f32[96,3072]{1,0:T(8,128)} %add.123), kind=kCustom, calls=%all-reduce-scatter.1 | all-reduce-scatter fusion | flops 393217 | bytes 1278464
  250.7 3.6 collective-permute-start.9
  265.9 7.6 %all-to-all-start.7 = ((bf16[16,2,3072]{2,1,0:T(2,128)(2,1)}), bf16[16,2,3072]{2,1,0:T(2,128)(2,1)S(1)}, u32[]{:S(2)}, u32[]{:S(2)}) async-start(bf16[16,2,3072]{2,1,0:T(2,128)(2,1)} %copy.57), calls=%async_computation.7 | async-start | bytes 393216 | tf_op jit(solution)/shard_map/all_to_all | solution.py:94
  275.2 6.9 %all-to-all-done.7 = bf16[16,2,3072]{2,1,0:T(2,128)(2,1)S(1)} async-done(((bf16[16,2,3072]{2,1,0:T(2,128)(2,1)}), bf16[16,2,3072]{2,1,0:T(2,128)(2,1)S(1)}, u32[]{:S(2)}, u32[]{:S(2)}) %all-to-all-start.7) | async-done | bytes 196640 | tf_op jit(solution)/shard_map/all_to_all | solution.py:94
  283.1 3.6 all-to-all-start.6
  286.9 4.0 %fusion.15 = f32[32,1024]{1,0:T(8,128)S(1)} fusion(bf16[32,3072]{1,0:T(8,128)(2,1)S(1)} %reshape.121, bf16[1,1,3072,1024]{3,2,1,0:T(8,128)(2,1)} %param.17), kind=kOutput, calls=%fused_computation.12 | convolution fusion | flops 201326592 | bytes 6619136 | tf_op jit(solution)/shard_map/dot_general | solution.py:21
  290.8 4.0 %fusion.69 = bf16[32,1024]{1,0:T(8,128)(2,1)S(1)} fusion(bf16[32,3072]{1,0:T(8,128)(2,1)S(1)} %reshape.121, bf16[1,1,3072,1024]{3,2,1,0:T(8,128)(2,1)} %param.18, f32[32,1024]{1,0:T(8,128)S(1)} %fusion.15), kind=kOutput, calls=%fused_computation.54 | convolution fusion | flops 201523200 | bytes 6684672 | tf_op jit(solution)/shard_map/dot_general | solution.py:22
  294.8 4.0 %fusion.3 = f32[16,2,3072]{2,0,1:T(8,128)S(1)} fusion(bf16[1,1,1024,3072]{3,2,1,0:T(8,128)(2,1)} %param.19, bf16[16,2,1024]{2,1,0:T(2,128)(2,1)S(1)} %dot_general.135), kind=kOutput, calls=%fused_computation | convolution fusion | flops 201326592 | bytes 6750208 | tf_op jit(solution)/shard_map/dot_general | solution.py:24
  299.9 6.0 %all-to-all-done.6 = bf16[16,6,3072]{2,1,0:T(8,128)(2,1)S(1)} async-done(((bf16[16,6,3072]{2,1,0:T(8,128)(2,1)}), bf16[16,6,3072]{2,1,0:T(8,128)(2,1)S(1)}, u32[]{:S(2)}, u32[]{:S(2)}) %all-to-all-start.6) | async-done | bytes 589856 | tf_op jit(solution)/shard_map/all_to_all | solution.py:82
  305.8 5.0 %all-to-all-start.8 = ((f32[16,2,3072]{2,1,0:T(2,128)}), f32[16,2,3072]{2,1,0:T(2,128)S(1)}, u32[]{:S(2)}, u32[]{:S(2)}) async-start(f32[16,2,3072]{2,1,0:T(2,128)} %copy.59), calls=%async_computation.8 | async-start | bytes 786432 | tf_op jit(solution)/shard_map/all_to_all | solution.py:97
  315.8 3.9 fusion.24
  325.4 49.6 %fusion.2 = f32[8,3072]{1,0:T(8,128)S(1)} fusion(f32[96,3072]{1,0:T(8,128)} %add.130), kind=kCustom, calls=%all-reduce-scatter.2 | all-reduce-scatter fusion | flops 393217 | bytes 1278464
  (199 shorter events, 99.5 us)
Async XLA Ops:
  5.3 17.0 %all-to-all-start.1 = ((bf16[16,2,3072]{2,1,0:T(2,128)(2,1)}), bf16[16,2,3072]{2,1,0:T(2,128)(2,1)S(1)}, u32[]{:S(2)}, u32[]{:S(2)}) async-start(bf16[16,2,3072]{2,1,0:T(2,128)(2,1)} %copy.46), calls=%async_computation.1 | async-start | bytes 393216 | tf_op jit(solution)/shard_map/all_to_all | solution.py:94
  15.2 119.5 %copy-start.25 = (f32[16,6]{0,1:T(8,128)}, f32[16,6]{0,1:T(8,128)S(1)}, u32[]{:S(2)}) copy-start(f32[16,6]{0,1:T(8,128)S(1)} %bitcast_subtract_fusion.1) | copy-start | bytes 1156
  23.2 22.7 %all-to-all-start = ((bf16[16,6,3072]{2,1,0:T(8,128)(2,1)}), bf16[16,6,3072]{2,1,0:T(8,128)(2,1)S(1)}, u32[]{:S(2)}, u32[]{:S(2)}) async-start(bf16[16,6,3072]{2,1,0:T(8,128)(2,1)} %stack.9), calls=%async_computation | async-start | bytes 1572864 | tf_op jit(solution)/shard_map/all_to_all | solution.py:82
  45.9 16.6 %all-to-all-start.2 = ((f32[16,2,3072]{2,1,0:T(2,128)}), f32[16,2,3072]{2,1,0:T(2,128)}, u32[]{:S(2)}, u32[]{:S(2)}) async-start(f32[16,2,3072]{2,1,0:T(2,128)} %copy.48), calls=%async_computation.2 | async-start | bytes 786432 | tf_op jit(solution)/shard_map/all_to_all | solution.py:97
  51.0 82.7 %copy-start.32 = (pred[6,8,24]{2,1,0:T(8,128)(4,1)}, pred[6,8,24]{2,1,0:T(8,128)(4,1)S(1)}, u32[]{:S(2)}) copy-start(pred[6,8,24]{2,1,0:T(8,128)(4,1)S(1)} %iota_compare_fusion) | copy-start | bytes 3460
  59.9 72.4 %copy-start.39 = (f32[6]{0:T(128)S(1)}, f32[6]{0:T(128)}, u32[]{:S(2)}) copy-start(f32[6]{0:T(128)} %copy-done.38) | copy-start | bytes 76
  59.9 74.7 %copy-start.15 = (bf16[1,6,3072]{2,0,1:T(2,128)(2,1)S(1)}, bf16[1,6,3072]{2,0,1:T(2,128)(2,1)}, u32[]{:S(2)}) copy-start(bf16[1,6,3072]{2,0,1:T(2,128)(2,1)} %get-tuple-element.13) | copy-start | bytes 110596
  64.0 78.4 %copy-start.17 = (bf16[1,3072,24]{1,2,0:T(8,128)(2,1)S(1)}, bf16[1,3072,24]{1,2,0:T(8,128)(2,1)}, u32[]{:S(2)}) copy-start(bf16[1,3072,24]{1,2,0:T(8,128)(2,1)} %param.13) | copy-start | bytes 442372
  115.1 12.6 %collective-permute-start.2 = (f32[8,3072]{1,0:T(8,128)S(1)}, f32[8,3072]{1,0:T(8,128)S(1)}, u32[]{:S(2)}, u32[]{:S(2)}) collective-permute-start(f32[8,3072]{1,0:T(8,128)S(1)} %fusion), channel_id=1, source_target_pairs={{0,1},{1,2},{2,3},{3,4},{4,5},{5,6},{6,7},{7,8},{8,9},{9,10},{10,1... | collective-permute-start | bytes 294920
  118.6 9.1 %collective-permute-start.3 = (f32[8,3072]{1,0:T(8,128)S(1)}, f32[8,3072]{1,0:T(8,128)S(1)}, u32[]{:S(2)}, u32[]{:S(2)}) collective-permute-start(f32[8,3072]{1,0:T(8,128)S(1)} %fusion), channel_id=1, source_target_pairs={{0,2},{1,3},{2,4},{3,5},{4,6},{5,7},{6,8},{7,9},{8,10},{9,11},{10,... | collective-permute-start | bytes 294920
  119.9 9.1 %collective-permute-start.4 = (f32[8,3072]{1,0:T(8,128)S(1)}, f32[8,3072]{1,0:T(8,128)}, u32[]{:S(2)}, u32[]{:S(2)}) collective-permute-start(f32[8,3072]{1,0:T(8,128)S(1)} %fusion), channel_id=1, source_target_pairs={{0,3},{1,4},{2,5},{3,6},{4,7},{5,8},{6,9},{7,10},{8,11},{9,12},{10... | collective-permute-start | bytes 294920
  121.9 5.8 %collective-permute-start.5 = (f32[6,3072]{1,0:T(8,128)S(1)}, f32[6,3072]{1,0:T(8,128)S(1)}, u32[]{:S(2)}, u32[]{:S(2)}) collective-permute-start(f32[6,3072]{1,0:T(8,128)S(1)} %slice.36), channel_id=1, source_target_pairs={{0,4},{1,5},{2,6},{3,7},{4,8},{5,9},{6,10},{7,11},{8,12},{9,13},{1... | collective-permute-start | bytes 221192
  132.4 2.2 collective-permute-start
  135.9 15.6 %all-to-all-start.4 = ((bf16[16,2,3072]{2,1,0:T(2,128)(2,1)}), bf16[16,2,3072]{2,1,0:T(2,128)(2,1)S(1)}, u32[]{:S(2)}, u32[]{:S(2)}) async-start(bf16[16,2,3072]{2,1,0:T(2,128)(2,1)} %copy.52), calls=%async_computation.4 | async-start | bytes 393216 | tf_op jit(solution)/shard_map/all_to_all | solution.py:94
  152.5 22.7 %all-to-all-start.3 = ((bf16[16,6,3072]{2,1,0:T(8,128)(2,1)}), bf16[16,6,3072]{2,1,0:T(8,128)(2,1)S(1)}, u32[]{:S(2)}, u32[]{:S(2)}) async-start(bf16[16,6,3072]{2,1,0:T(8,128)(2,1)} %stack.10), calls=%async_computation.3 | async-start | bytes 1572864 | tf_op jit(solution)/shard_map/all_to_all | solution.py:82
  175.2 16.6 %all-to-all-start.5 = ((f32[16,2,3072]{2,1,0:T(2,128)}), f32[16,2,3072]{2,1,0:T(2,128)S(1)}, u32[]{:S(2)}, u32[]{:S(2)}) async-start(f32[16,2,3072]{2,1,0:T(2,128)} %copy.54), calls=%async_computation.5 | async-start | bytes 786432 | tf_op jit(solution)/shard_map/all_to_all | solution.py:97
  189.0 70.5 %copy-start.12 = (bf16[6,3072]{1,0:T(8,128)(2,1)S(1)}, bf16[6,3072]{1,0:T(8,128)(2,1)}, u32[]{:S(2)}) copy-start(bf16[6,3072]{1,0:T(8,128)(2,1)} %copy-done.11) | copy-start | bytes 110596
  193.1 80.4 %copy-start.18 = (bf16[1,3072,24]{1,2,0:T(8,128)(2,1)S(1)}, bf16[1,3072,24]{1,2,0:T(8,128)(2,1)}, u32[]{:S(2)}) copy-start(bf16[1,3072,24]{1,2,0:T(8,128)(2,1)} %param.13) | copy-start | bytes 442372
  244.3 12.2 %collective-permute-start.6 = (f32[8,3072]{1,0:T(8,128)S(1)}, f32[8,3072]{1,0:T(8,128)S(1)}, u32[]{:S(2)}, u32[]{:S(2)}) collective-permute-start(f32[8,3072]{1,0:T(8,128)S(1)} %fusion.1), channel_id=1, source_target_pairs={{0,1},{1,2},{2,3},{3,4},{4,5},{5,6},{6,7},{7,8},{8,9},{9,10},{10,1... | collective-permute-start | bytes 294920
  247.5 9.0 %collective-permute-start.7 = (f32[8,3072]{1,0:T(8,128)S(1)}, f32[8,3072]{1,0:T(8,128)S(1)}, u32[]{:S(2)}, u32[]{:S(2)}) collective-permute-start(f32[8,3072]{1,0:T(8,128)S(1)} %fusion.1), channel_id=1, source_target_pairs={{0,2},{1,3},{2,4},{3,5},{4,6},{5,7},{6,8},{7,9},{8,10},{9,11},{10,... | collective-permute-start | bytes 294920
  248.8 8.4 %collective-permute-start.8 = (f32[8,3072]{1,0:T(8,128)S(1)}, f32[8,3072]{1,0:T(8,128)}, u32[]{:S(2)}, u32[]{:S(2)}) collective-permute-start(f32[8,3072]{1,0:T(8,128)S(1)} %fusion.1), channel_id=1, source_target_pairs={{0,3},{1,4},{2,5},{3,6},{4,7},{5,8},{6,9},{7,10},{8,11},{9,12},{10... | collective-permute-start | bytes 294920
  250.7 5.8 %collective-permute-start.9 = (f32[6,3072]{1,0:T(8,128)S(1)}, f32[6,3072]{1,0:T(8,128)S(1)}, u32[]{:S(2)}, u32[]{:S(2)}) collective-permute-start(f32[6,3072]{1,0:T(8,128)S(1)} %slice.37), channel_id=1, source_target_pairs={{0,4},{1,5},{2,6},{3,7},{4,8},{5,9},{6,10},{7,11},{8,12},{9,13},{1... | collective-permute-start | bytes 221192
  260.4 2.6 collective-permute-start.1
  265.9 16.2 %all-to-all-start.7 = ((bf16[16,2,3072]{2,1,0:T(2,128)(2,1)}), bf16[16,2,3072]{2,1,0:T(2,128)(2,1)S(1)}, u32[]{:S(2)}, u32[]{:S(2)}) async-start(bf16[16,2,3072]{2,1,0:T(2,128)(2,1)} %copy.57), calls=%async_computation.7 | async-start | bytes 393216 | tf_op jit(solution)/shard_map/all_to_all | solution.py:94
  283.1 22.7 %all-to-all-start.6 = ((bf16[16,6,3072]{2,1,0:T(8,128)(2,1)}), bf16[16,6,3072]{2,1,0:T(8,128)(2,1)S(1)}, u32[]{:S(2)}, u32[]{:S(2)}) async-start(bf16[16,6,3072]{2,1,0:T(8,128)(2,1)} %stack.11), calls=%async_computation.6 | async-start | bytes 1572864 | tf_op jit(solution)/shard_map/all_to_all | solution.py:82
  305.8 16.5 %all-to-all-start.8 = ((f32[16,2,3072]{2,1,0:T(2,128)}), f32[16,2,3072]{2,1,0:T(2,128)S(1)}, u32[]{:S(2)}, u32[]{:S(2)}) async-start(f32[16,2,3072]{2,1,0:T(2,128)} %copy.59), calls=%async_computation.8 | async-start | bytes 786432 | tf_op jit(solution)/shard_map/all_to_all | solution.py:97
  319.7 70.8 %copy-start.8 = (bf16[2,6,3072]{2,1,0:T(8,128)(2,1)S(1)}, bf16[2,6,3072]{2,1,0:T(8,128)(2,1)}, u32[]{:S(2)}) copy-start(bf16[2,6,3072]{2,1,0:T(8,128)(2,1)} %copy-done.7) | copy-start | bytes 221188
  319.7 70.8 %copy-start.10 = (bf16[6,3072]{1,0:T(8,128)(2,1)S(1)}, bf16[6,3072]{1,0:T(8,128)(2,1)}, u32[]{:S(2)}) copy-start(bf16[6,3072]{1,0:T(8,128)(2,1)} %copy-done.9) | copy-start | bytes 110596
  375.0 12.5 %collective-permute-start.10 = (f32[8,3072]{1,0:T(8,128)S(1)}, f32[8,3072]{1,0:T(8,128)S(1)}, u32[]{:S(2)}, u32[]{:S(2)}) collective-permute-start(f32[8,3072]{1,0:T(8,128)S(1)} %fusion.2), channel_id=1, source_target_pairs={{0,1},{1,2},{2,3},{3,4},{4,5},{5,6},{6,7},{7,8},{8,9},{9,10},{10,1... | collective-permute-start | bytes 294920
  378.5 9.0 %collective-permute-start.11 = (f32[8,3072]{1,0:T(8,128)S(1)}, f32[8,3072]{1,0:T(8,128)S(1)}, u32[]{:S(2)}, u32[]{:S(2)}) collective-permute-start(f32[8,3072]{1,0:T(8,128)S(1)} %fusion.2), channel_id=1, source_target_pairs={{0,2},{1,3},{2,4},{3,5},{4,6},{5,7},{6,8},{7,9},{8,10},{9,11},{10,... | collective-permute-start | bytes 294920
  379.8 8.3 %collective-permute-start.12 = (f32[8,3072]{1,0:T(8,128)S(1)}, f32[8,3072]{1,0:T(8,128)}, u32[]{:S(2)}, u32[]{:S(2)}) collective-permute-start(f32[8,3072]{1,0:T(8,128)S(1)} %fusion.2), channel_id=1, source_target_pairs={{0,3},{1,4},{2,5},{3,6},{4,7},{5,8},{6,9},{7,10},{8,11},{9,12},{10... | collective-permute-start | bytes 294920
  381.7 5.7 %collective-permute-start.13 = (f32[6,3072]{1,0:T(8,128)S(1)}, f32[6,3072]{1,0:T(8,128)S(1)}, u32[]{:S(2)}, u32[]{:S(2)}) collective-permute-start(f32[6,3072]{1,0:T(8,128)S(1)} %slice.38), channel_id=1, source_target_pairs={{0,4},{1,5},{2,6},{3,7},{4,8},{5,9},{6,10},{7,11},{8,12},{9,13},{1... | collective-permute-start | bytes 221192
  (34 other events, 695.7 us)
